TPU v7x, 256 devices: a whole 4x4x8 slice. The times are simulated.
256 devices in a mesh: seq: 32 (over x, z), head: 8 (over y, core).
Axes of the slice: x: 4, y: 4, z: 8, core: 2. Of those that a mesh axis runs over, the one named last changes fastest.
Arguments:
- inner_input: bfloat16 [16384, 16384], P('seq', 'head'), may hold values from -6 to 6
- state_input: bfloat16 [16384, 4096], P('seq', 'head'), may hold values from -6 to 6
- gate_input: bfloat16 [16384, 16384], P('seq', 'head'), may hold values from -6 to 6
- inner_taps: bfloat16 [4, 16384], P(None, 'head'), may hold values from -3 to 3
- inner_bias: bfloat16 [16384], P('head'), may hold values from -3 to 3
- state_taps: bfloat16 [4, 4096], P(None, 'head'), may hold values from -3 to 3
- state_bias: bfloat16 [4096], P('head'), may hold values from -3 to 3
- step_raw: float32 [256, 16384], P('head', 'seq'), may hold values from -5.3 to -1
- step_bias: float32 [256], P('head'), may hold values from -0.5 to 0.5
- decay_log: float32 [256], P('head'), may hold values from -9 to 1.26
- skip_gain: float32 [256], P('head'), may hold values from 0.5 to 1.5
- norm_gain: bfloat16 [16384], P('head'), may hold values from 0.5 to 1.5
- out_weight: bfloat16 [16384, 4096], P('head', 'seq'), may hold values from -0.09375 to 0.09375
- sequence_lengths: int32 [4], replicated, may hold values from 1 to 8192, 16384 in all
Outputs:
- mixed_out: bfloat16 [16384, 4096], P('seq', 'head')
Inputs may be any that keep to these rules, and one draw needn't show every extreme that they name: `sequence_lengths`: the 4 sequences lie end to end in the order given and fill all 16384 positions; the longest has exactly 8192 positions.
All inputs are finite; a program needn't handle non-finite values.
Results may differ from a plain program's by a relative error of at most 0.018.
Values may be sent and summed in bfloat16 or wider, within the bound.
No kernel may reach another device: no remote copies, remote signals or barrier semaphores. Data moves between devices by JAX's collectives and lax.ppermute only.
A program may use at most 256 MiB of HBM per device.

v0:
```python
import jax
import jax.numpy as jnp
import numpy as np
from jax import lax
from jax.sharding import Mesh
from jax.sharding import PartitionSpec as P

HEAD_DIM = 64
STATE_DIM = 256
BLOCK_LEN = 256
HIGHEST = lax.Precision.HIGHEST
EPSILON = 1e-05
SEQ = ("sx", "sz")


def segment_of(positions, sequence_lengths):
    starts = jnp.cumsum(sequence_lengths) - sequence_lengths
    hits = (positions[:, None] >= starts[None, :]).astype(jnp.int32)
    return jnp.sum(hits, axis=1) - 1


def causal_conv(extended, seg_extended, tap_table, bias_row):
    tap_count = tap_table.shape[0]
    length = extended.shape[0] - tap_count + 1
    current = seg_extended[tap_count - 1 :]
    summed = jnp.zeros((length, bias_row.shape[0]), jnp.float32) + bias_row.astype(jnp.float32)
    for start_shift in range(tap_count):
        kept_mask = (seg_extended[start_shift : start_shift + length] == current).astype(
            jnp.float32
        )
        summed = (
            summed
            + tap_table[start_shift].astype(jnp.float32)
            * extended[start_shift : start_shift + length].astype(jnp.float32)
            * kept_mask[:, None]
        )
    return jax.nn.silu(summed).astype(jnp.bfloat16)


def exclusive_weights(factors, place):
    n = factors.shape[0]
    idx = jnp.arange(n)
    j = idx[:, None]
    t = idx[None, :]
    between = (t > j) & (t < place)
    prods = jnp.prod(jnp.where(between[:, :, None], factors[None, :, :], 1.0), axis=1)
    return jnp.where((idx < place)[:, None], prods, 0.0)


def pack_state(state, factor):
    heads = factor.shape[0]
    flat = state.reshape(-1, state.shape[-1])
    extra = jnp.zeros((8, flat.shape[1]), jnp.float32).at[0, :heads].set(factor)
    return jnp.concatenate([flat, extra], axis=0).astype(jnp.bfloat16)


def unpack_state(gathered, heads):
    rows = gathered.shape[1] - 8
    states = (
        gathered[:, :rows]
        .astype(jnp.float32)
        .reshape(gathered.shape[0], heads, rows // heads, gathered.shape[2])
    )
    factors = gathered[:, rows, :heads].astype(jnp.float32)
    return (states, factors)


def combine(states, factors, place):
    weights = exclusive_weights(factors, place)
    return jnp.sum(weights[:, :, None, None] * states, axis=0)


def per_device(
    inner_input,
    state_input,
    gate_input,
    inner_taps,
    inner_bias,
    state_taps,
    state_bias,
    step_raw,
    step_bias,
    decay_log,
    skip_gain,
    norm_gain,
    out_weight,
    sequence_lengths,
):
    tok_rows = inner_input.shape[0]
    inner_width = inner_input.shape[1]
    heads = step_raw.shape[0]
    groups = state_input.shape[1] // (2 * STATE_DIM)
    per_group = heads // groups
    tap_count = inner_taps.shape[0]
    chunks = tok_rows // BLOCK_LEN
    L = BLOCK_LEN
    nz = lax.axis_size("sz")
    nseq = lax.axis_size("sx") * nz
    place = lax.axis_index("sx") * nz + lax.axis_index("sz")
    first_row = place * tok_rows
    weights = lax.all_gather(out_weight, SEQ, axis=1, tiled=True)
    positions = first_row + lax.iota(jnp.int32, tok_rows + tap_count - 1) - (tap_count - 1)
    seg_extended = segment_of(positions, sequence_lengths)
    seg_local = seg_extended[tap_count - 1 :]
    seg_before = seg_extended[tap_count - 2]
    tail_rows = jnp.concatenate(
        [inner_input[tok_rows - tap_count + 1 :], state_input[tok_rows - tap_count + 1 :]], axis=1
    )
    received = lax.ppermute(tail_rows, SEQ, [(s, s + 1) for s in range(nseq - 1)])
    inner_conv = causal_conv(
        jnp.concatenate([received[:, :inner_width], inner_input]),
        seg_extended,
        inner_taps,
        inner_bias,
    )
    state_conv = causal_conv(
        jnp.concatenate([received[:, inner_width:], state_input]),
        seg_extended,
        state_taps,
        state_bias,
    )
    u = inner_conv.reshape(chunks, L, groups, per_group, HEAD_DIM)
    vectors = state_conv.reshape(chunks, L, groups, 2, STATE_DIM)
    write_b = vectors[:, :, :, 0]
    read_c = vectors[:, :, :, 1]
    steps = jax.nn.softplus(step_raw + step_bias[:, None]).reshape(groups, per_group, chunks, L)
    rates = jnp.exp(decay_log).reshape(groups, per_group)
    gains = skip_gain.reshape(groups, per_group)
    running = jnp.cumsum(-rates[..., None, None] * steps, axis=3)
    seg_c = seg_local.reshape(chunks, L)
    seg_prev = jnp.concatenate([seg_before[None], seg_c[:-1, L - 1]])
    alive = (seg_c == seg_prev[:, None]).astype(jnp.float32)
    last = running[..., L - 1 :]
    u32 = u.astype(jnp.float32)
    scaled = u32 * jnp.transpose(steps, (2, 3, 0, 1))[..., None]
    closing = (seg_c == seg_c[:, L - 1 :]).astype(jnp.float32) * jnp.exp(last - running)
    weighted = scaled * jnp.transpose(closing, (2, 3, 0, 1))[..., None]
    chunk_states = jnp.einsum(
        "cjghp,cjgn->cghpn", weighted, write_b.astype(jnp.float32), precision=HIGHEST
    )
    kept = alive[:, L - 1] * jnp.exp(last[..., 0])
    kept = jnp.transpose(kept, (2, 0, 1))
    shard_state = chunk_states[0]
    shard_factor = kept[0]
    for c in range(1, chunks):
        shard_state = kept[c][..., None, None] * shard_state + chunk_states[c]
        shard_factor = shard_factor * kept[c]
    packed, weights = lax.optimization_barrier(
        (pack_state(shard_state, shard_factor.reshape(-1)), weights)
    )
    row = lax.all_gather(packed, "sz")
    row_states, row_factors = unpack_state(row, heads)
    zpos = lax.axis_index("sz")
    in_row = combine(row_states, row_factors, zpos)
    row_decay = jnp.prod(jnp.where((jnp.arange(nz) < zpos)[:, None], row_factors, 1.0), axis=0)
    row_total = combine(row_states, row_factors, nz)
    row_total_factor = jnp.prod(row_factors, axis=0)
    rows = lax.all_gather(pack_state(row_total, row_total_factor), "sx")
    rows_states, rows_factors = unpack_state(rows, heads)
    before_rows = combine(rows_states, rows_factors, lax.axis_index("sx"))
    state_in = (row_decay[:, None, None] * before_rows + in_row).reshape(
        groups, per_group, HEAD_DIM, STATE_DIM
    )
    read32 = read_c.astype(jnp.float32)
    scores = jnp.einsum("cign,cjgn->gcij", read_c, write_b, preferred_element_type=jnp.float32)
    row_index = lax.broadcasted_iota(jnp.int32, (L, L), 0)
    col_index = lax.broadcasted_iota(jnp.int32, (L, L), 1)
    linked = (row_index >= col_index)[None] & (seg_c[:, :, None] == seg_c[:, None, :])
    spread = running[..., :, None] - running[..., None, :]
    decays = jnp.where(linked, jnp.exp(jnp.where(linked, spread, 0.0)), 0.0)
    within = jnp.einsum("ghcij,cjghp->cighp", decays * scores[:, None], scaled, precision=HIGHEST)
    entering = [state_in]
    for c in range(1, chunks):
        entering.append(kept[c - 1][..., None, None] * entering[-1] + chunk_states[c - 1])
    entering = jnp.stack(entering)
    carried = jnp.einsum("cign,cghpn->cighp", read32, entering, precision=HIGHEST)
    enter_scale = jnp.transpose(alive[None, None] * jnp.exp(running), (2, 3, 0, 1))
    outputs = within + carried * enter_scale[..., None] + gains[..., None] * u32
    y_all = outputs.reshape(tok_rows, groups, per_group * HEAD_DIM)
    gated = y_all * jax.nn.silu(gate_input.astype(jnp.float32)).reshape(
        tok_rows, groups, per_group * HEAD_DIM
    )
    mean_sq = jnp.mean(gated * gated, axis=2, keepdims=True)
    gain_rows = norm_gain.astype(jnp.float32).reshape(groups, per_group * HEAD_DIM)
    normed = (
        (gated * lax.rsqrt(mean_sq + EPSILON) * gain_rows)
        .astype(jnp.bfloat16)
        .reshape(tok_rows, inner_width)
    )
    partial_out = jnp.dot(normed, weights, preferred_element_type=jnp.float32)
    return lax.psum_scatter(
        partial_out.astype(jnp.bfloat16), "head", scatter_dimension=1, tiled=True
    )


def split_seq(mesh):
    seq_devices = mesh.devices[:, 0]
    try:
        nx = len({d.coords[0] for d in seq_devices})
    except AttributeError:
        nx = 1
    nseq = seq_devices.shape[0]
    return Mesh(mesh.devices.reshape(nx, nseq // nx, mesh.devices.shape[1]), ("sx", "sz", "head"))


def solution(mesh):
    inner = split_seq(mesh)
    in_specs = (
        P(SEQ, "head"),
        P(SEQ, "head"),
        P(SEQ, "head"),
        P(None, "head"),
        P("head"),
        P(None, "head"),
        P("head"),
        P("head", SEQ),
        P("head"),
        P("head"),
        P("head"),
        P("head"),
        P("head", SEQ),
        P(),
    )
    out_specs = P(SEQ, "head")
    return jax.shard_map(
        per_device, mesh=inner, in_specs=in_specs, out_specs=out_specs, check_vma=False
    )
```

profile of v0, /device:TPU:2, one launch (start us, length us, event | category | flops | bytes accessed | tf_op | source)
XLA Modules:
  0.0 402.9 jit_solution(4032910775150019644)
XLA Ops:
  8.8 3.8 collective-permute-start
  18.5 1.3 pad_add_fusion
  24.0 2.9 copy.134
  28.1 6.8 %fusion.31 = f32[512,2048]{0,1:T(8,128)} fusion(bf16[512,2048]{0,1:T(8,128)(2,1)S(1)} %copy.134, f32[2048]{0:T(1024)S(1)} %bitcast.130, f32[512]{0:T(512)S(1)} %get-tuple-element.54, bf16[3,2048]{0,1:T(8,128)(2,1)S(1)} %copy.133, f32[2048]{0:T(1024)S(1)} %bitcast.131, f32[512]{0:T(512)S(1)} %get-tuple-element.55, f32[2048]{0:T(1024)S(1)} %bitcast.129, ...), kind=kLoop, calls=%fused_computation.54 | loop fusion | flops 31457280 | bytes 6350848 | tf_op jit(solution)/shard_map/convert_element_type | solution.py:134
  34.9 5.9 %reshape.740 = f32[2,256,32,64]{1,0,3,2:T(2,128)} reshape(f32[512,2048]{0,1:T(8,128)} %fusion.31) | data formatting | bytes 8388608 | tf_op jit(solution)/shard_map/convert_element_type | solution.py:134
  42.6 9.1 %broadcast_multiply_fusion = (f32[2,256,32,64]{1,0,3,2:T(2,128)S(1)}, f32[2,256,32,64]{1,0,3,2:T(2,128)}) fusion(f32[2,256,32]{1,0,2:T(2,128)S(1)} %copy.147, f32[2,256,32,64]{1,0,3,2:T(2,128)} %reshape.740, f32[2,256,32]{1,0,2:T(2,128)S(1)} %bitcast.126), kind=kLoop, calls=%fused_computation.52 | loop fusion | flops 2097152 | bytes 12713984 | tf_op jit(solution)/shard_map/mul | solution.py:137
  51.7 2.1 fusion.22
  53.8 1.9 copy-done
  57.0 104.4 %all-gather.5.cloned.1.call-done = bf16[2048,4096]{1,0:T(8,128)(2,1)} async-done(((bf16[2048,128]{1,0:T(8,128)(2,1)}), bf16[2048,4096]{1,0:T(8,128)(2,1)}) %all-gather.5.cloned.1.call-update) | async-done | bytes 16777232 | tf_op jit(solution)/shard_map/all_gather | solution.py:101
  161.8 93.9 %all-gather.9.cloned.1.call-done = bf16[16448,256]{1,0:T(8,128)(2,1)} async-done(((bf16[2056,256]{1,0:T(8,128)(2,1)}), bf16[16448,256]{1,0:T(8,128)(2,1)}) %all-gather.9.cloned.1.call-update) | async-done | bytes 8421392 | tf_op jit(solution)/shard_map/all_gather | solution.py:151
  258.3 11.2 %fusion = (bf16[2048,256]{1,0:T(8,128)(2,1)S(1)}, f32[2048,256]{1,0:T(8,128)S(1)}) fusion(f32[8,2048]{1,0:T(8,128)S(1)} %mul.520, bf16[8,2056,256]{2,1,0:T(8,128)(2,1)} %bitcast.122, f32[8,2048]{1,0:T(8,128)} %mul.529), kind=kLoop, calls=%fused_computation.2 | loop fusion | flops 19922944 | bytes 11665408 | tf_op jit(solution)/shard_map/reduce_sum | solution.py:70
  274.0 4.0 copy.154
  278.2 6.1 %reshape.746 = f32[2,256,1,32,64]{1,0,4,3,2:T(2,128)} reshape(f32[512,2048]{0,1:T(8,128)} %fusion.31) | data formatting | bytes 8388608 | tf_op jit(solution)/shard_map/convert_element_type | solution.py:134
  284.5 21.5 %fusion.2 = f32[2,32,64,256]{3,2,1,0:T(8,128)} fusion(f32[2,256,256]{2,1,0:T(8,128)S(1)} %fusion.37, f32[32,2,256]{2,0,1:T(8,128)S(1)} %reduce_window_sum.47, pred[2,256,256]{2,1,0:T(8,128)(4,1)S(1)} %compare_and_fusion, f32[2,256,32,64]{1,0,3,2:T(2,128)} %get-tuple-element.40), kind=kOutput, calls=%fused_computation.4 | convolution fusion | flops 3238002688 | bytes 9109504 | tf_op jit(solution)/shard_map/ghcij,cjghp->cighp/dot_general | solution.py:171
  306.0 13.5 %all-gather.7.cloned.1.call-done = bf16[4,2056,256]{2,1,0:T(8,128)(2,1)} async-done(((bf16[1,2056,256]{2,1,0:T(8,128)(2,1)}), bf16[4,2056,256]{2,1,0:T(8,128)(2,1)}) %all-gather.7.cloned.1.call-update) | async-done | bytes 4210704 | tf_op jit(solution)/shard_map/all_gather | solution.py:158
  320.6 3.2 multiply_reduce_fusion
  324.1 1.9 copy-done.1
  326.4 1.8 copy-done.2
  328.2 1.3 copy-done.4
  329.4 3.0 fusion.21
  332.5 3.3 copy.153
  337.4 1.4 multiply_reduce_fusion.1
  338.9 15.8 %convolution_convert_fusion = bf16[512,4096]{1,0:T(8,128)(2,1)} fusion(bf16[2048,4096]{1,0:T(8,128)(2,1)} %all-gather.5.cloned.1.call-done, f32[2048]{0:T(1024)S(1)} %convert_element_type.187, f32[512]{0:T(512)S(1)} %add_rsqrt_fusion, f32[512,2048]{0,1:T(8,128)S(1)} %bitcast.119, bf16[512,2048]{0,1:T(8,128)(2,1)S(1)} %copy-done.3), kind=kOutput, calls=%fused_computation.16 | convolution fusion | flops 8601468928 | bytes 27273216 | tf_op jit(solution)/shard_map/dot_general | solution.py:190
  354.6 41.7 %reduce-scatter.2.cloned.1.call-done = bf16[512,512]{1,0:T(8,128)(2,1)} async-done(((bf16[512,4096]{1,0:T(8,128)(2,1)}), bf16[512,512]{1,0:T(8,128)(2,1)}) %reduce-scatter.2.cloned.1.call-update) | async-done | bytes 524304 | tf_op jit(solution)/shard_map/reduce_scatter | solution.py:191
  (115 shorter events, 27.5 us)
Async XLA Ops:
  6.5 21.1 %copy-start.9 = (bf16[2048]{0:T(1024)(128)(2,1)S(1)}, bf16[2048]{0:T(1024)(128)(2,1)}, u32[]{:S(2)}) copy-start(bf16[2048]{0:T(1024)(128)(2,1)} %param.22) | copy-start | bytes 12292
  6.5 21.2 %copy-start.12 = (bf16[512]{0:T(512)(128)(2,1)S(1)}, bf16[512]{0:T(512)(128)(2,1)}, u32[]{:S(2)}) copy-start(bf16[512]{0:T(512)(128)(2,1)} %param.24) | copy-start | bytes 3076
  6.5 154.9 %all-gather.5.cloned.1.call-start = ((), (), s32[]{:S(2)}) async-start(), calls=%async_computation.1 | async-start | bytes 17301504 | tf_op jit(solution)/shard_map/all_gather | solution.py:101
  7.3 248.5 %all-gather.9.cloned.1.call-start = ((), (), s32[]{:S(2)}) async-start(), calls=%async_computation.4 | async-start | bytes 9474048 | tf_op jit(solution)/shard_map/all_gather | solution.py:151
  8.8 18.9 %collective-permute-start = (bf16[3,2560]{1,0:T(4,128)(2,1)S(1)}, bf16[3,2560]{1,0:T(4,128)(2,1)S(1)}, u32[]{:S(2)}, u32[]{:S(2)}) collective-permute-start(bf16[3,2560]{1,0:T(4,128)(2,1)S(1)} %pad_maximum_fusion.3), channel_id=1, source_target_pairs={{0,8},{8,16},{16,24},{24,32},{32,40},{40,48},{48,56},{56,64},{64,7... | collective-permute-start | bytes 46088 | tf_op jit(solution)/shard_map/ppermute | solution.py:109
  34.9 6.0 %copy-start.5 = (bf16[512,512]{1,0:T(8,128)(2,1)S(1)}, bf16[512,512]{1,0:T(8,128)(2,1)}, u32[]{:S(2)}) copy-start(bf16[512,512]{1,0:T(8,128)(2,1)} %param.19) | copy-start | bytes 1572868
  40.8 1.8 copy-start.6
  53.7 1.9 copy-start
  161.5 158.0 %all-gather.7.cloned.1.call-start = ((), (), s32[]{:S(2)}) async-start(), calls=%async_computation.2 | async-start | bytes 5263360 | tf_op jit(solution)/shard_map/all_gather | solution.py:158
  270.5 125.8 %reduce-scatter.2.cloned.1.call-start = ((), (), s32[]{:S(2)}) async-start(), calls=%async_computation.3 | async-start | bytes 4718592 | tf_op jit(solution)/shard_map/reduce_scatter | solution.py:191
  273.9 4.0 copy-start.7
  306.0 17.8 %copy-start.8 = (f32[32]{0:T(128)S(1)}, f32[32]{0:T(128)}, u32[]{:S(2)}) copy-start(f32[32]{0:T(128)} %get-tuple-element.61) | copy-start | bytes 388
  323.8 2.2 copy-start.1
  323.8 2.2 copy-start.11
  326.0 2.2 copy-start.2
  326.0 3.5 copy-start.4
  326.0 3.5 copy-start.10
  335.8 1.6 copy-start.3
Sparse Core Ops, SparseCore 0:
  9.8 151.6 all-gather.4
  163.3 92.4 all-gather.8
  270.6 48.8 all-gather.6
  354.8 41.5 reduce-scatter.1
where the time goes:
time: 404 us; the launch traced here: 403 us
  waiting for transfers between devices  254 us (63%)
  other arithmetic  47.9 us (12%)
  matrix products  42.6 us (11%)
  local copies, waits for them, and re-layouts  40.3 us (10%)
  between operations  13.6 us (3%)
  starting transfers between devices  4.13 us (1%)
    all_gather x1, waiting for transfers between devices, per_device(): weights = lax.all_gather(out_weight, SEQ, axis=1, tiled=True)  104 us
    all_gather x1, waiting for transfers between devices, per_device(): row = lax.all_gather(packed, 'sz')  93.9 us
    reduce_scatter x1, waiting for transfers between devices, per_device(): lax.psum_scatter(partial_out.astype(jnp.bfloat16), 'head', scatter_dimens...  41.7 us
    dot_general x1, matrix products, per_device(): jnp.einsum('ghcij,cjghp->cighp', decays * scores[:, None], scaled, precis...  21.5 us
    dot_general x1, matrix products, per_device(): partial_out = jnp.dot(normed, weights, preferred_element_type=jnp.float32)  15.8 us
    unnamed x29, local copies, waits for them, and re-layouts  15.3 us
    reduce_sum x2, other arithmetic, combine(): return jnp.sum(weights[:, :, None, None] * states, axis=0)  14.4 us
    all_gather x1, waiting for transfers between devices, per_device(): rows = lax.all_gather(pack_state(row_total, row_total_factor), 'sx')  13.5 us
  transfers between devices with their start and end apart: 5, of which 4 were waited for; matrix products, arithmetic and copies ran while one was open for 20% of the time, Pallas kernels for 0%

commit v1 on v0

--- a/solution.py
+++ b/solution.py
@@ -98,7 +98,11 @@
     nseq = lax.axis_size("sx") * nz
     place = lax.axis_index("sx") * nz + lax.axis_index("sz")
     first_row = place * tok_rows
-    weights = lax.all_gather(out_weight, SEQ, axis=1, tiled=True)
+    load_pages_here = lambda dim_no, device_axis, block_here: jnp.concatenate(
+        lax.all_to_all(jnp.stack([block_here] * lax.psum(1, device_axis)), device_axis, 0, 0),
+        dim_no,
+    )
+    weights = load_pages_here(1, SEQ, block_here=out_weight)
     positions = first_row + lax.iota(jnp.int32, tok_rows + tap_count - 1) - (tap_count - 1)
     seg_extended = segment_of(positions, sequence_lengths)
     seg_local = seg_extended[tap_count - 1 :]

time: 404 us -> 709 us (1.75)
  waiting for transfers between devices: 254 us -> 539 us
  starting transfers between devices: 4.13 us -> 15.5 us
  local copies, waits for them, and re-layouts: 40.3 us -> 49 us
    ppermute x1, waiting for transfers between devices: 0.01 us -> 391 us  [per_device(): lax.ppermute(tail_rows, SEQ, [(s, s + 1) for s in range(nseq - 1)])]
    all_gather x1 -> x0, waiting for transfers between devices: 104 us -> none  [per_device(): weights = lax.all_gather(out_weight, SEQ, axis=1, tiled=True)]
    all_to_all x0 -> x1, starting transfers between devices: none -> 11.8 us  [per_device(): lax.all_to_all(jnp.stack([block_here] * lax.psum(1, device_axis)), device...]
    another operation x10 -> x11, local copies, waits for them, and re-layouts: 2.94 us -> 10.4 us  [the longest x1 5.96 us: per_device(): jnp.stack([block_here] * lax.psum(1, device_axis))]
    unnamed x29 -> x70, local copies, waits for them, and re-layouts: 15.3 us -> 17.2 us
  transfers between devices with their start and end apart: 5 -> 5, of which waited for: 4 -> 4; matrix products, arithmetic and copies ran while one was open for 20% -> 11% of each run, Pallas kernels for 0% -> 0%
where the time goes in v1:
time: 709 us; the launch traced here: 708 us
  waiting for transfers between devices  539 us (76%)
  local copies, waits for them, and re-layouts  49 us (7%)
  other arithmetic  46.5 us (7%)
  matrix products  43.7 us (6%)
  starting transfers between devices  15.5 us (2%)
  between operations  13.8 us (2%)
    ppermute x1, waiting for transfers between devices, per_device(): lax.ppermute(tail_rows, SEQ, [(s, s + 1) for s in range(nseq - 1)])  391 us
    all_gather x1, waiting for transfers between devices, per_device(): row = lax.all_gather(packed, 'sz')  94.1 us
    reduce_scatter x1, waiting for transfers between devices, per_device(): lax.psum_scatter(partial_out.astype(jnp.bfloat16), 'head', scatter_dimens...  41.7 us
    dot_general x1, matrix products, per_device(): jnp.einsum('ghcij,cjghp->cighp', decays * scores[:, None], scaled, precis...  21.5 us
    unnamed x70, local copies, waits for them, and re-layouts  17.2 us
    dot_general x1, matrix products, per_device(): partial_out = jnp.dot(normed, weights, preferred_element_type=jnp.float32)  16.8 us
    reduce_sum x2, other arithmetic, combine(): return jnp.sum(weights[:, :, None, None] * states, axis=0)  14.4 us
  transfers between devices with their start and end apart: 5, of which 4 were waited for; matrix products, arithmetic and copies ran while one was open for 11% of the time, Pallas kernels for 0%

profile of v1, /device:TPU:2, one launch (start us, length us, event | category | flops | bytes accessed | tf_op | source)
XLA Modules:
  0.0 707.6 jit_solution(1846150978261678530)
XLA Ops:
  7.8 6.0 stack.6
  13.8 11.8 %all-to-all-start = ((bf16[32,2048,128]{1,2,0:T(8,128)(2,1)}), bf16[32,2048,128]{1,2,0:T(8,128)(2,1)}, u32[]{:S(2)}, u32[]{:S(2)}) async-start(bf16[32,2048,128]{1,2,0:T(8,128)(2,1)} %stack.6), calls=%async_computation | async-start | bytes 33554432 | tf_op jit(solution)/shard_map/all_to_all | solution.py:102
  26.5 3.4 collective-permute-start
  38.6 2.9 copy.139
  43.5 391.4 %collective-permute-done = bf16[3,2560]{1,0:T(4,128)(2,1)S(1)} collective-permute-done((bf16[3,2560]{1,0:T(4,128)(2,1)S(1)}, bf16[3,2560]{1,0:T(4,128)(2,1)S(1)}, u32[]{:S(2)}, u32[]{:S(2)}) %collective-permute-start) | collective-permute-done | bytes 15392 | tf_op jit(solution)/shard_map/ppermute | solution.py:113
  435.8 7.5 %fusion.31 = f32[512,2048]{0,1:T(8,128)} fusion(bf16[512,2048]{0,1:T(8,128)(2,1)S(1)} %copy.139, f32[2048]{0:T(1024)} %bitcast.133, f32[512]{0:T(512)} %get-tuple-element.54, bf16[3,2048]{0,1:T(8,128)(2,1)S(1)} %copy.138, f32[2048]{0:T(1024)} %bitcast.134, f32[512]{0:T(512)} %get-tuple-element.55, f32[2048]{0:T(1024)} %bitcast.132, ...), kind=kLoop, calls=%fused_computation.54 | loop fusion | flops 31457280 | bytes 6350848 | tf_op jit(solution)/shard_map/convert_element_type | solution.py:138
  443.4 5.9 reshape.750
  451.1 9.0 %broadcast_multiply_fusion = (f32[2,256,32,64]{1,0,3,2:T(2,128)S(1)}, f32[2,256,32,64]{1,0,3,2:T(2,128)}) fusion(f32[2,256,32]{1,0,2:T(2,128)S(1)} %copy.152, f32[2,256,32,64]{1,0,3,2:T(2,128)} %reshape.750, f32[2,256,32]{1,0,2:T(2,128)S(1)} %bitcast.129), kind=kLoop, calls=%fused_computation.52 | loop fusion | flops 2097152 | bytes 12713984 | tf_op jit(solution)/shard_map/mul | solution.py:141
  460.1 2.1 fusion.22
  462.2 1.9 copy-done
  465.8 94.1 %all-gather.6.cloned.1.call-done = bf16[16448,256]{1,0:T(8,128)(2,1)} async-done(((bf16[2056,256]{1,0:T(8,128)(2,1)}), bf16[16448,256]{1,0:T(8,128)(2,1)}) %all-gather.6.cloned.1.call-update) | async-done | bytes 8421392 | tf_op jit(solution)/shard_map/all_gather | solution.py:155
  561.8 11.2 %fusion = (bf16[2048,256]{1,0:T(8,128)(2,1)S(1)}, f32[2048,256]{1,0:T(8,128)S(1)}) fusion(f32[8,2048]{1,0:T(8,128)S(1)} %mul.520, bf16[8,2056,256]{2,1,0:T(8,128)(2,1)} %bitcast.125, f32[8,2048]{1,0:T(8,128)} %mul.529), kind=kLoop, calls=%fused_computation.2 | loop fusion | flops 19922944 | bytes 11665408 | tf_op jit(solution)/shard_map/reduce_sum | solution.py:70
  576.7 1.5 reshape.731
  578.3 4.0 copy.160
  583.2 6.1 reshape.756
  589.6 21.5 %fusion.2 = f32[2,32,64,256]{3,2,1,0:T(8,128)} fusion(f32[2,256,256]{2,1,0:T(8,128)S(1)} %fusion.37, f32[32,2,256]{2,0,1:T(8,128)S(1)} %reduce_window_sum.47, pred[2,256,256]{2,1,0:T(8,128)(4,1)S(1)} %compare_and_fusion, f32[2,256,32,64]{1,0,3,2:T(2,128)} %get-tuple-element.40), kind=kOutput, calls=%fused_computation.4 | convolution fusion | flops 3238002688 | bytes 9109504 | tf_op jit(solution)/shard_map/ghcij,cjghp->cighp/dot_general | solution.py:175
  611.1 12.0 %all-gather.4.cloned.1.call-done = bf16[4,2056,256]{2,1,0:T(8,128)(2,1)} async-done(((bf16[1,2056,256]{2,1,0:T(8,128)(2,1)}), bf16[4,2056,256]{2,1,0:T(8,128)(2,1)}) %all-gather.4.cloned.1.call-update) | async-done | bytes 4210704 | tf_op jit(solution)/shard_map/all_gather | solution.py:162
  624.1 3.2 multiply_reduce_fusion
  627.7 1.9 copy-done.1
  630.0 1.8 copy-done.2
  633.0 3.0 fusion.21
  636.1 3.4 copy.159
  642.5 16.8 %convolution_convert_fusion = bf16[512,4096]{1,0:T(8,128)(2,1)} fusion(bf16[2048,4096]{0,1:T(8,128)(2,1)} %bitcast.33, f32[2048]{0:T(1024)S(1)} %convert_element_type.187, f32[512]{0:T(512)S(1)} %add_rsqrt_fusion, f32[512,2048]{0,1:T(8,128)S(1)} %bitcast.122, bf16[512,2048]{0,1:T(8,128)(2,1)} %copy.160), kind=kOutput, calls=%fused_computation.16 | convolution fusion | flops 8601468928 | bytes 27273216 | tf_op jit(solution)/shard_map/dot_general | solution.py:194
  659.3 41.7 %reduce-scatter.2.cloned.1.call-done = bf16[512,512]{1,0:T(8,128)(2,1)} async-done(((bf16[512,4096]{1,0:T(8,128)(2,1)}), bf16[512,512]{1,0:T(8,128)(2,1)}) %reduce-scatter.2.cloned.1.call-update) | async-done | bytes 524304 | tf_op jit(solution)/shard_map/reduce_scatter | solution.py:195
  (157 shorter events, 29.9 us)
Async XLA Ops:
  13.7 12.7 %copy-start.5 = (bf16[512,512]{1,0:T(8,128)(2,1)S(1)}, bf16[512,512]{1,0:T(8,128)(2,1)}, u32[]{:S(2)}) copy-start(bf16[512,512]{1,0:T(8,128)(2,1)} %param.19) | copy-start | bytes 1572868
  13.8 16.2 %copy-start.31 = (s32[4]{0:T(128)S(1)}, s32[4]{0:T(128)}, u32[]{:S(2)}) copy-start(s32[4]{0:T(128)} %param.31) | copy-start | bytes 52
  13.8 17.1 %copy-start.8 = (f32[32,512]{1,0:T(8,128)S(1)}, f32[32,512]{1,0:T(8,128)}, u32[]{:S(2)}) copy-start(f32[32,512]{1,0:T(8,128)} %param.25) | copy-start | bytes 196612
  13.8 17.1 %copy-start.30 = (f32[32]{0:T(128)S(1)}, f32[32]{0:T(128)}, u32[]{:S(2)}) copy-start(f32[32]{0:T(128)} %param.26) | copy-start | bytes 388
  13.8 17.3 %copy-start.32 = (f32[32]{0:T(128)S(1)}, f32[32]{0:T(128)}, u32[]{:S(2)}) copy-start(f32[32]{0:T(128)} %param.27) | copy-start | bytes 388
  13.8 22.7 %copy-start.18 = (bf16[4,512]{1,0:T(4,128)(2,1)S(1)}, bf16[4,512]{1,0:T(4,128)(2,1)}, u32[]{:S(2)}) copy-start(bf16[4,512]{1,0:T(4,128)(2,1)} %param.23) | copy-start | bytes 12292
  13.8 23.6 %copy-start.9 = (bf16[4,2048]{1,0:T(4,128)(2,1)S(1)}, bf16[4,2048]{1,0:T(4,128)(2,1)}, u32[]{:S(2)}) copy-start(bf16[4,2048]{1,0:T(4,128)(2,1)} %param.21) | copy-start | bytes 49156
  13.8 451.7 %all-to-all-start = ((bf16[32,2048,128]{1,2,0:T(8,128)(2,1)}), bf16[32,2048,128]{1,2,0:T(8,128)(2,1)}, u32[]{:S(2)}, u32[]{:S(2)}) async-start(bf16[32,2048,128]{1,2,0:T(8,128)(2,1)} %stack.6), calls=%async_computation | async-start | bytes 33554432 | tf_op jit(solution)/shard_map/all_to_all | solution.py:102
  25.6 16.7 %copy-start.24 = (bf16[2048]{0:T(1024)(128)(2,1)S(1)}, bf16[2048]{0:T(1024)(128)(2,1)}, u32[]{:S(2)}) copy-start(bf16[2048]{0:T(1024)(128)(2,1)} %param.22) | copy-start | bytes 12292
  25.6 17.3 %copy-start.29 = (bf16[512]{0:T(512)(128)(2,1)S(1)}, bf16[512]{0:T(512)(128)(2,1)}, u32[]{:S(2)}) copy-start(bf16[512]{0:T(512)(128)(2,1)} %param.24) | copy-start | bytes 3076
  25.6 534.2 %all-gather.6.cloned.1.call-start = ((), (), s32[]{:S(2)}) async-start(), calls=%async_computation.4 | async-start | bytes 9474048 | tf_op jit(solution)/shard_map/all_gather | solution.py:155
  26.5 408.4 %collective-permute-start = (bf16[3,2560]{1,0:T(4,128)(2,1)S(1)}, bf16[3,2560]{1,0:T(4,128)(2,1)S(1)}, u32[]{:S(2)}, u32[]{:S(2)}) collective-permute-start(bf16[3,2560]{1,0:T(4,128)(2,1)S(1)} %pad_maximum_fusion.3), channel_id=1, source_target_pairs={{0,8},{8,16},{16,24},{24,32},{32,40},{40,48},{48,56},{56,64},{64,7... | collective-permute-start | bytes 46088 | tf_op jit(solution)/shard_map/ppermute | solution.py:113
  32.4 402.4 %copy-start.10 = (s32[2,256]{1,0:T(2,128)}, s32[2,256]{1,0:T(2,128)S(1)}, u32[]{:S(2)}) copy-start(s32[2,256]{1,0:T(2,128)S(1)} %eq.58) | copy-start | bytes 6148
  443.4 5.9 copy-start.14
  443.4 5.9 copy-start.15
  443.4 5.9 copy-start.19
  443.4 5.9 copy-start.20
  443.4 5.9 copy-start.21
  443.4 5.9 copy-start.22
  443.4 5.9 copy-start.23
  465.5 157.6 %all-gather.4.cloned.1.call-start = ((), (), s32[]{:S(2)}) async-start(), calls=%async_computation.2 | async-start | bytes 5263360 | tf_op jit(solution)/shard_map/all_gather | solution.py:162
  561.8 13.0 %copy-start.17 = (f32[32,2,2]{0,1,2:T(2,128)S(1)}, f32[32,2,2]{0,1,2:T(2,128)}, u32[]{:S(2)}) copy-start(f32[32,2,2]{0,1,2:T(2,128)} %copy-done.16) | copy-start | bytes 1540
  573.0 10.0 %copy-start.11 = (s32[2,256]{1,0:T(2,128)S(1)}, s32[2,256]{1,0:T(2,128)}, u32[]{:S(2)}) copy-start(s32[2,256]{1,0:T(2,128)} %copy-done.10) | copy-start | bytes 6148
  574.1 126.9 %reduce-scatter.2.cloned.1.call-start = ((), (), s32[]{:S(2)}) async-start(), calls=%async_computation.3 | async-start | bytes 4718592 | tf_op jit(solution)/shard_map/reduce_scatter | solution.py:195
  (15 other events, 45.4 us)
Sparse Core Ops, SparseCore 0:
  465.6 94.1 all-gather.5
  574.2 48.8 all-gather.3
  659.5 41.5 reduce-scatter.1
